TPU v7x, 32 devices: a whole 2x2x4 slice. The times are simulated.
32 devices in a mesh: grp: 4 (over y, x), tp: 8 (over z, core).
Axes of the slice: x: 2, y: 2, z: 4, core: 2. Of those that a mesh axis runs over, the one named last changes fastest.
Arguments:
- tokens: bfloat16 [1280, 4096], P(('grp', 'tp')), may hold values from -6 to 6
- norm_gain: float32 [4096], replicated, may hold values from 0.5 to 1.5
- spill_blocks: int32 [1], replicated, may hold values from 0 to 7, as said below
- image_gate: bfloat16 [4096, 11008], P('grp', 'tp'), may hold values from -0.09375 to 0.09375
- image_up: bfloat16 [4096, 11008], P('grp', 'tp'), may hold values from -0.09375 to 0.09375
- image_down: bfloat16 [11008, 4096], P('tp', 'grp'), may hold values from -0.0546875 to 0.0546875
- text_gate: bfloat16 [4096, 11008], P(None, 'tp'), may hold values from -0.09375 to 0.09375
- text_up: bfloat16 [4096, 11008], P(None, 'tp'), may hold values from -0.09375 to 0.09375
- text_down: bfloat16 [11008, 4096], P('tp'), may hold values from -0.0546875 to 0.0546875
Outputs:
- mixed: bfloat16 [1280, 4096], P(('grp', 'tp'))
Inputs may be any that keep to these rules, and one draw needn't show every extreme that they name: `spill_blocks`: 1 distinct indices of 0 to 8 - 1, in increasing order.
All inputs are finite; a program needn't handle non-finite values.
Results may differ from a plain program's by a relative error of at most 0.0046.
Values may be sent and summed in bfloat16 or wider, within the bound.
A program may use at most 256 MiB of HBM per device.

v0:
```python
import jax
import jax.numpy as jnp
from jax import lax
from jax.sharding import PartitionSpec as P

norm_epsilon = 1e-05
bf16 = jnp.bfloat16
f32 = jnp.float32


def on_device(
    tokens, norm_gain, spill_blocks, image_gate, image_up, image_down, text_gate, text_up, text_down
):
    rows, width = tokens.shape
    n_tp = lax.axis_size("tp")
    n_grp = lax.axis_size("grp")
    group = lax.axis_index("grp")
    n_spill = spill_blocks.shape[0]
    in_text = group == n_grp - 1
    kslice = image_gate.shape[0]
    units = image_gate.shape[1]
    wide = tokens.astype(f32)
    scale = lax.rsqrt(jnp.mean(wide * wide, axis=-1, keepdims=True) + norm_epsilon)
    normed = (wide * scale * norm_gain).astype(bf16)
    cols = normed.reshape(rows, n_grp, kslice).transpose(1, 0, 2)
    cols = lax.all_to_all(cols, "grp", 0, 0, tiled=True)
    cols = lax.all_gather(cols, "tp", axis=1, tiled=False)
    image_part = cols[: n_grp - 1].reshape(-1, kslice)
    spill_part = cols[n_grp - 1][spill_blocks].reshape(-1, kslice)
    x = jnp.concatenate([image_part, spill_part], axis=0)
    n_rows = x.shape[0]
    step = 16 * n_grp
    padded = (n_rows + step - 1) // step * step
    x = jnp.pad(x, ((0, padded - n_rows), (0, 0)))
    part_gate = jnp.dot(x, image_gate, preferred_element_type=f32).astype(bf16)
    part_up = jnp.dot(x, image_up, preferred_element_type=f32).astype(bf16)
    gate = lax.psum_scatter(part_gate, "grp", scatter_dimension=0, tiled=True)
    up = lax.psum_scatter(part_up, "grp", scatter_dimension=0, tiled=True)
    piece = lax.all_gather(normed, "tp", axis=0, tiled=True)

    def text_ffn():
        g = jnp.dot(piece, text_gate, preferred_element_type=f32)
        u = jnp.dot(piece, text_up, preferred_element_type=f32)
        h = (jax.nn.silu(g) * u).astype(bf16)
        return jnp.dot(h, text_down, preferred_element_type=f32).astype(bf16)

    text_terms = lax.cond(in_text, text_ffn, lambda: jnp.zeros((n_tp * rows, width), bf16))
    text_out = lax.psum_scatter(text_terms, "tp", scatter_dimension=0, tiled=True)
    hidden = (jax.nn.silu(gate.astype(f32)) * up.astype(f32)).astype(bf16)
    hidden = lax.all_gather(hidden, "grp", axis=0, tiled=True)
    terms = jnp.dot(hidden, image_down, preferred_element_type=f32).astype(bf16)
    image_terms = terms[: (n_grp - 1) * n_tp * rows].reshape(n_grp - 1, n_tp, rows, kslice)
    spill_terms = terms[(n_grp - 1) * n_tp * rows : n_rows].reshape(n_spill, rows, kslice)
    placed = jnp.zeros((n_tp, rows, kslice), bf16).at[spill_blocks].set(spill_terms)
    every = jnp.concatenate([image_terms, placed[None]], axis=0).transpose(1, 0, 2, 3)
    mine = lax.psum_scatter(every.reshape(n_tp, -1, kslice), "tp", scatter_dimension=0, tiled=True)
    mine = mine.reshape(n_grp, rows, kslice)
    back = lax.all_to_all(mine, "grp", 0, 0, tiled=True)
    branch = back.transpose(1, 0, 2).reshape(rows, width)
    is_spill = jnp.any(lax.axis_index("tp") == spill_blocks)
    use_text = jnp.logical_and(in_text, jnp.logical_not(is_spill))
    branch = jnp.where(use_text, text_out, branch)
    return (wide + branch.astype(f32)).astype(bf16)


def solution(mesh):
    in_specs = (
        P(("grp", "tp"), None),
        P(),
        P(),
        P("grp", "tp"),
        P("grp", "tp"),
        P("tp", "grp"),
        P(None, "tp"),
        P(None, "tp"),
        P("tp", None),
    )
    out_specs = P(("grp", "tp"), None)
    return jax.shard_map(
        on_device, mesh=mesh, in_specs=in_specs, out_specs=out_specs, check_vma=False
    )
```

profile of v0, /device:TPU:0, one launch (start us, length us, event | category | flops | bytes accessed | tf_op | source)
XLA Modules:
  0.0 316.9 jit_solution(15081478361410944292)
XLA Ops:
  6.5 1.3 fusion.10
  7.8 1.1 fusion.12
  9.3 11.6 %all_to_all.10 = bf16[4,40,1024]{2,1,0:T(8,128)(2,1)S(1)} all-to-all(bf16[4,40,1024]{2,1,0:T(8,128)(2,1)S(1)} %copy.27), channel_id=1, replica_groups=mesh['grp'=4,'tp'=8] {'grp'}, dimensions={0} | all-to-all | bytes 655360 | tf_op jit(solution)/shard_map/all_to_all | solution.py:26
  20.9 1.0 copy.28
  22.6 32.7 %all-gather.9.cloned.1.call-done = bf16[4,320,1024]{2,0,1:T(4,128)(2,1)} async-done(((bf16[4,40,1024]{2,0,1:T(4,128)(2,1)}), bf16[4,320,1024]{2,0,1:T(4,128)(2,1)}) %all-gather.9.cloned.1.call-update) | async-done | bytes 2621456 | tf_op jit(solution)/shard_map/all_gather | solution.py:27
  55.3 3.4 %slice.47 = bf16[1,320,1024]{2,0,1:T(2,128)(2,1)S(1)} slice(bf16[4,320,1024]{2,0,1:T(4,128)(2,1)} %all-gather.9.cloned.1.call-done), slice={[3:4], [0:320], [0:1024]} | slice | bytes 1310720 | tf_op jit(solution)/shard_map/slice | solution.py:29
  59.7 1.3 copy-done.5
  61.0 5.0 %convolution_convert_fusion.2 = bf16[1024,1376]{0,1:T(8,128)(2,1)} fusion(bf16[1024,1376]{0,1:T(8,128)(2,1)S(1)} %copy-done, bf16[40,1024]{1,0:T(8,128)(2,1)S(1)} %dynamic-slice_bitcast_fusion, bf16[960,1024]{1,0:T(8,128)(2,1)S(1)} %bitcast.35), kind=kOutput, calls=%fused_computation.8 | convolution fusion | flops 2894430208 | bytes 7684096 | tf_op jit(solution)/shard_map/dot_general | solution.py:35
  66.1 1.5 copy-done.6
  67.6 6.9 %convolution_convert_fusion.1 = bf16[1024,1376]{0,1:T(8,128)(2,1)} fusion(bf16[1024,1376]{0,1:T(8,128)(2,1)} %param.17, bf16[40,1024]{1,0:T(8,128)(2,1)S(1)} %dynamic-slice_bitcast_fusion, bf16[960,1024]{1,0:T(8,128)(2,1)S(1)} %bitcast.36), kind=kOutput, calls=%fused_computation.7 | convolution fusion | flops 2894430208 | bytes 7684096 | tf_op jit(solution)/shard_map/dot_general | solution.py:36
  74.5 32.0 %reduce-scatter.7.cloned.1.call-done = bf16[256,1376]{0,1:T(8,128)(2,1)} async-done(((bf16[1024,1376]{0,1:T(8,128)(2,1)}), bf16[256,1376]{0,1:T(8,128)(2,1)}) %reduce-scatter.7.cloned.1.call-update) | async-done | bytes 704528 | tf_op jit(solution)/shard_map/reduce_scatter | solution.py:37
  106.5 44.3 %reduce-scatter.9.cloned.1.call-done = bf16[256,1376]{0,1:T(8,128)(2,1)} async-done(((bf16[1024,1376]{0,1:T(8,128)(2,1)}), bf16[256,1376]{0,1:T(8,128)(2,1)}) %reduce-scatter.9.cloned.1.call-update) | async-done | bytes 704528 | tf_op jit(solution)/shard_map/reduce_scatter | solution.py:38
  150.8 2.6 fusion.9
  154.8 39.8 %all-gather.7.cloned.1.call-done = bf16[1024,1376]{0,1:T(8,128)(2,1)} async-done(((bf16[256,1376]{0,1:T(8,128)(2,1)}), bf16[1024,1376]{0,1:T(8,128)(2,1)}) %all-gather.7.cloned.1.call-update) | async-done | bytes 2818064 | tf_op jit(solution)/shard_map/all_gather | solution.py:50
  194.6 6.1 %convolution_convert_fusion.3 = bf16[1024,1024]{1,0:T(8,128)(2,1)S(1)} fusion(bf16[1024,1376]{0,1:T(8,128)(2,1)} %all-gather.7.cloned.1.call-done, bf16[1376,1024]{1,0:T(8,128)(2,1)} %param.18), kind=kOutput, calls=%fused_computation.11 | convolution fusion | flops 2886729728 | bytes 7733248 | tf_op jit(solution)/shard_map/dot_general | solution.py:51
  201.6 1.9 pad_maximum_fusion
  203.5 26.3 %all-gather.5.cloned.1.call-done = bf16[320,4096]{1,0:T(8,128)(2,1)} async-done(((bf16[40,4096]{1,0:T(8,128)(2,1)}), bf16[320,4096]{1,0:T(8,128)(2,1)}) %all-gather.5.cloned.1.call-update) | async-done | bytes 2621456 | tf_op jit(solution)/shard_map/all_gather | solution.py:39
  229.8 1.8 conditional.1
  229.8 1.8 broadcast.40
  231.6 37.3 %reduce-scatter.11.cloned.1.call-done = bf16[1,160,1024]{2,1,0:T(8,128)(2,1)} async-done(((bf16[8,160,1024]{2,1,0:T(8,128)(2,1)}), bf16[1,160,1024]{2,1,0:T(8,128)(2,1)}) %reduce-scatter.11.cloned.1.call-update) | async-done | bytes 327696 | tf_op jit(solution)/shard_map/reduce_scatter | solution.py:56
  268.9 3.7 %all-to-all-start.1 = ((bf16[4,40,1024]{2,1,0:T(8,128)(2,1)}), bf16[4,40,1024]{2,1,0:T(8,128)(2,1)S(1)}, u32[]{:S(2)}, u32[]{:S(2)}) async-start(bf16[4,40,1024]{2,1,0:T(8,128)(2,1)} %bitcast.41), calls=%async_computation.5 | async-start | bytes 655360 | tf_op jit(solution)/shard_map/all_to_all | solution.py:58
  272.7 5.5 %all-to-all-done.1 = bf16[4,40,1024]{2,1,0:T(8,128)(2,1)S(1)} async-done(((bf16[4,40,1024]{2,1,0:T(8,128)(2,1)}), bf16[4,40,1024]{2,1,0:T(8,128)(2,1)S(1)}, u32[]{:S(2)}, u32[]{:S(2)}) %all-to-all-start.1) | async-done | bytes 327712 | tf_op jit(solution)/shard_map/all_to_all | solution.py:58
  279.0 29.3 %reduce-scatter.5.cloned.1.call-done = bf16[40,4096]{1,0:T(8,128)(2,1)} async-done(((bf16[320,4096]{1,0:T(8,128)(2,1)}), bf16[40,4096]{1,0:T(8,128)(2,1)}) %reduce-scatter.5.cloned.1.call-update) | async-done | bytes 327696 | tf_op jit(solution)/shard_map/reduce_scatter | solution.py:48
  308.2 1.8 fusion.13
  (39 shorter events, 4.6 us)
Async XLA Ops:
  6.5 54.5 %copy-start = (bf16[1024,1376]{0,1:T(8,128)(2,1)S(1)}, bf16[1024,1376]{0,1:T(8,128)(2,1)}, u32[]{:S(2)}) copy-start(bf16[1024,1376]{0,1:T(8,128)(2,1)} %param.16) | copy-start | bytes 8454148
  6.5 48.8 %all-gather.9.cloned.1.call-start = ((), (), s32[]{:S(2)}) async-start(), calls=%async_computation.12 | async-start | bytes 2949120 | tf_op jit(solution)/shard_map/all_gather | solution.py:27
  9.0 49.7 %copy-start.3 = (bf16[40,4096]{1,0:T(8,128)(2,1)}, bf16[40,4096]{1,0:T(8,128)(2,1)S(1)}, u32[]{:S(2)}) copy-start(bf16[40,4096]{1,0:T(8,128)(2,1)S(1)} %fusion.12) | copy-start | bytes 983044
  21.9 84.6 %reduce-scatter.7.cloned.1.call-start = ((), (), s32[]{:S(2)}) async-start(), calls=%async_computation.8 | async-start | bytes 3522560 | tf_op jit(solution)/shard_map/reduce_scatter | solution.py:37
  55.3 3.6 %copy-start.2 = (bf16[4,320,1024]{2,0,1:T(4,128)(2,1)S(1)}, bf16[4,320,1024]{2,0,1:T(4,128)(2,1)}, u32[]{:S(2)}) copy-start(bf16[4,320,1024]{2,0,1:T(4,128)(2,1)} %all-gather.9.cloned.1.call-done) | copy-start | bytes 7864324
  59.7 1.3 copy-start.5
  66.0 1.5 copy-start.6
  66.0 84.7 %reduce-scatter.9.cloned.1.call-start = ((), (), s32[]{:S(2)}) async-start(), calls=%async_computation.9 | async-start | bytes 3522560 | tf_op jit(solution)/shard_map/reduce_scatter | solution.py:38
  74.4 79.6 %copy-start.7 = (s32[3]{0:T(128)S(1)}, s32[3]{0:T(128)}, u32[]{:S(2)}) copy-start(s32[3]{0:T(128)} %constant.55.clone.1) | copy-start | bytes 40
  74.4 120.1 %all-gather.7.cloned.1.call-start = ((), (), s32[]{:S(2)}) async-start(), calls=%async_computation.10 | async-start | bytes 3522560 | tf_op jit(solution)/shard_map/all_gather | solution.py:50
  153.4 76.4 %all-gather.5.cloned.1.call-start = ((), (), s32[]{:S(2)}) async-start(), calls=%async_computation.6 | async-start | bytes 2949120 | tf_op jit(solution)/shard_map/all_gather | solution.py:39
  154.0 114.9 %reduce-scatter.11.cloned.1.call-start = ((), (), s32[]{:S(2)}) async-start(), calls=%async_computation.11 | async-start | bytes 2949120 | tf_op jit(solution)/shard_map/reduce_scatter | solution.py:56
  203.5 104.7 %reduce-scatter.5.cloned.1.call-start = ((), (), s32[]{:S(2)}) async-start(), calls=%async_computation.7 | async-start | bytes 2949120 | tf_op jit(solution)/shard_map/reduce_scatter | solution.py:48
  231.6 76.6 %copy-start.4 = (bf16[40,4096]{1,0:T(8,128)(2,1)S(1)}, bf16[40,4096]{1,0:T(8,128)(2,1)}, u32[]{:S(2)}) copy-start(bf16[40,4096]{1,0:T(8,128)(2,1)} %param.13) | copy-start | bytes 983044
  231.6 78.4 %copy-start.1 = (bf16[1024,1376]{0,1:T(8,128)(2,1)S(1)}, bf16[1024,1376]{0,1:T(8,128)(2,1)}, u32[]{:S(2)}) copy-start(bf16[1024,1376]{0,1:T(8,128)(2,1)} %param.16) | copy-start | bytes 8454148
  268.9 9.3 %all-to-all-start.1 = ((bf16[4,40,1024]{2,1,0:T(8,128)(2,1)}), bf16[4,40,1024]{2,1,0:T(8,128)(2,1)S(1)}, u32[]{:S(2)}, u32[]{:S(2)}) async-start(bf16[4,40,1024]{2,1,0:T(8,128)(2,1)} %bitcast.41), calls=%async_computation.5 | async-start | bytes 655360 | tf_op jit(solution)/shard_map/all_to_all | solution.py:58
Sparse Core Ops, SparseCore 0:
  22.1 33.2 all-gather.8
  66.2 40.3 reduce-scatter.6
  109.6 41.1 reduce-scatter.8
  153.5 41.0 all-gather.6
  196.1 33.6 all-gather.4
  231.9 36.9 reduce-scatter.10
  271.2 36.9 reduce-scatter.4
where the time goes:
time: 317 us
  waiting for transfers between devices  248 us (78%)
  matrix products  18 us (6%)
  between operations  14.3 us (5%)
  blocking collectives  11.6 us (4%)
  local copies, waits for them, and re-layouts  11.2 us (4%)
  other arithmetic  10.1 us (3%)
  starting transfers between devices  3.99 us (1%)
    reduce_scatter x1, waiting for transfers between devices, on_device(): up = lax.psum_scatter(part_up, 'grp', scatter_dimension=0, tiled=True)  44.3 us
    all_gather x1, waiting for transfers between devices, on_device(): hidden = lax.all_gather(hidden, 'grp', axis=0, tiled=True)  39.8 us
    reduce_scatter x1, waiting for transfers between devices, on_device(): lax.psum_scatter(every.reshape(n_tp, -1, kslice), 'tp', scatter_dimension...  37.3 us
    all_gather x1, waiting for transfers between devices, on_device(): cols = lax.all_gather(cols, 'tp', axis=1, tiled=False)  32.7 us
    reduce_scatter x1, waiting for transfers between devices, on_device(): gate = lax.psum_scatter(part_gate, 'grp', scatter_dimension=0, tiled=True)  32 us
    reduce_scatter x1, waiting for transfers between devices, on_device(): lax.psum_scatter(text_terms, 'tp', scatter_dimension=0, tiled=True)  29.3 us
    all_gather x1, waiting for transfers between devices, on_device(): piece = lax.all_gather(normed, 'tp', axis=0, tiled=True)  26.3 us
    all_to_all x1, blocking collectives, on_device(): cols = lax.all_to_all(cols, 'grp', 0, 0, tiled=True)  11.6 us
  transfers between devices with their start and end apart: 8, of which 8 were waited for; matrix products, arithmetic and copies ran while one was open for 6% of the time, Pallas kernels for 0%

commit v1 on v0

--- a/solution.py
+++ b/solution.py
@@ -36,7 +36,12 @@
     part_up = jnp.dot(x, image_up, preferred_element_type=f32).astype(bf16)
     gate = lax.psum_scatter(part_gate, "grp", scatter_dimension=0, tiled=True)
     up = lax.psum_scatter(part_up, "grp", scatter_dimension=0, tiled=True)
-    piece = lax.all_gather(normed, "tp", axis=0, tiled=True)
+    ring = [normed]
+    for hop in range(7):
+        ring.append(lax.ppermute(ring[-1], "tp", [(dev, (dev + 1) % 8) for dev in range(8)]))
+    piece = jnp.roll(
+        jnp.concatenate(ring[::-1], axis=0), (lax.axis_index("tp") + 1) * ring[0].shape[0], axis=0
+    )
 
     def text_ffn():
         g = jnp.dot(piece, text_gate, preferred_element_type=f32)

time: 317 us -> 290 us (0.915)
  waiting for transfers between devices: 248 us -> 209 us
  local copies, waits for them, and re-layouts: 11.2 us -> 20.3 us
    ppermute x0 -> x7, waiting for transfers between devices: none -> 48.8 us  [on_device(): lax.ppermute(ring[-1], 'tp', [(dev, (dev + 1) % 8) for dev in range(8)])]
    all_gather x1, waiting for transfers between devices: 39.8 us -> 3.29 us  [on_device(): hidden = lax.all_gather(hidden, 'grp', axis=0, tiled=True)]
    all_gather x1 -> x0, waiting for transfers between devices: 26.3 us -> none  [on_device(): piece = lax.all_gather(normed, 'tp', axis=0, tiled=True)]
    reduce_scatter x1, waiting for transfers between devices: 32 us -> 16.6 us  [on_device(): gate = lax.psum_scatter(part_gate, 'grp', scatter_dimension=0, tiled=True)]
    unnamed x18 -> x50, local copies, waits for them, and re-layouts: 3.73 us -> 12.8 us
    reduce_scatter x1, waiting for transfers between devices: 37.3 us -> 28.2 us  [on_device(): lax.psum_scatter(every.reshape(n_tp, -1, kslice), 'tp', scatter_dimension...]
  transfers between devices with their start and end apart: 8 -> 14, of which waited for: 8 -> 13; matrix products, arithmetic and copies ran while one was open for 6% -> 9% of each run, Pallas kernels for 0% -> 0%
where the time goes in v1:
time: 290 us; the launch traced here: 289 us
  waiting for transfers between devices  209 us (72%)
  local copies, waits for them, and re-layouts  20.3 us (7%)
  matrix products  18.3 us (6%)
  between operations  14.3 us (5%)
  other arithmetic  11.7 us (4%)
  blocking collectives  11.6 us (4%)
  starting transfers between devices  4.19 us (1%)
    ppermute x7, waiting for transfers between devices, on_device(): lax.ppermute(ring[-1], 'tp', [(dev, (dev + 1) % 8) for dev in range(8)])  48.8 us
    reduce_scatter x1, waiting for transfers between devices, on_device(): up = lax.psum_scatter(part_up, 'grp', scatter_dimension=0, tiled=True)  44.3 us
    all_gather x1, waiting for transfers between devices, on_device(): cols = lax.all_gather(cols, 'tp', axis=1, tiled=False)  32.7 us
    reduce_scatter x1, waiting for transfers between devices, on_device(): lax.psum_scatter(text_terms, 'tp', scatter_dimension=0, tiled=True)  29.3 us
    reduce_scatter x1, waiting for transfers between devices, on_device(): lax.psum_scatter(every.reshape(n_tp, -1, kslice), 'tp', scatter_dimension...  28.2 us
    reduce_scatter x1, waiting for transfers between devices, on_device(): gate = lax.psum_scatter(part_gate, 'grp', scatter_dimension=0, tiled=True)  16.6 us
    unnamed x50, local copies, waits for them, and re-layouts  12.8 us
    all_to_all x1, blocking collectives, on_device(): cols = lax.all_to_all(cols, 'grp', 0, 0, tiled=True)  11.6 us
  transfers between devices with their start and end apart: 14, of which 13 were waited for; matrix products, arithmetic and copies ran while one was open for 9% of the time, Pallas kernels for 0%

profile of v1, /device:TPU:0, one launch (start us, length us, event | category | flops | bytes accessed | tf_op | source)
XLA Modules:
  0.0 289.2 jit_solution(699832604901520293)
XLA Ops:
  9.3 11.6 %all_to_all.10 = bf16[4,40,1024]{2,1,0:T(8,128)(2,1)S(1)} all-to-all(bf16[4,40,1024]{2,1,0:T(8,128)(2,1)S(1)} %copy.27), channel_id=1, replica_groups=mesh['grp'=4,'tp'=8] {'grp'}, dimensions={0} | all-to-all | bytes 655360 | tf_op jit(solution)/shard_map/all_to_all | solution.py:26
  22.6 32.7 %all-gather.6.cloned.1.call-done = bf16[4,320,1024]{2,0,1:T(4,128)(2,1)} async-done(((bf16[4,40,1024]{2,0,1:T(4,128)(2,1)}), bf16[4,320,1024]{2,0,1:T(4,128)(2,1)}) %all-gather.6.cloned.1.call-update) | async-done | bytes 2621456 | tf_op jit(solution)/shard_map/all_gather | solution.py:27
  55.3 3.4 %slice.47 = bf16[1,320,1024]{2,0,1:T(2,128)(2,1)S(1)} slice(bf16[4,320,1024]{2,0,1:T(4,128)(2,1)} %all-gather.6.cloned.1.call-done), slice={[3:4], [0:320], [0:1024]} | slice | bytes 1310720 | tf_op jit(solution)/shard_map/slice | solution.py:29
  60.9 5.0 %convolution_convert_fusion.2 = bf16[1024,1376]{0,1:T(8,128)(2,1)} fusion(bf16[1024,1376]{0,1:T(8,128)(2,1)S(1)} %copy-done, bf16[40,1024]{1,0:T(8,128)(2,1)S(1)} %dynamic-slice_bitcast_fusion, bf16[960,1024]{1,0:T(8,128)(2,1)S(1)} %bitcast.33), kind=kOutput, calls=%fused_computation.18 | convolution fusion | flops 2894430208 | bytes 7684096 | tf_op jit(solution)/shard_map/dot_general | solution.py:35
  66.0 7.1 %convolution_convert_fusion.1 = bf16[1024,1376]{0,1:T(8,128)(2,1)} fusion(bf16[1024,1376]{0,1:T(8,128)(2,1)} %param.17, bf16[40,1024]{1,0:T(8,128)(2,1)S(1)} %dynamic-slice_bitcast_fusion, bf16[960,1024]{1,0:T(8,128)(2,1)} %bitcast.34), kind=kOutput, calls=%fused_computation.17 | convolution fusion | flops 2894430208 | bytes 7684096 | tf_op jit(solution)/shard_map/dot_general | solution.py:36
  73.5 8.1 %collective-permute-done = bf16[40,4096]{1,0:T(8,128)(2,1)S(1)} collective-permute-done((bf16[40,4096]{1,0:T(8,128)(2,1)S(1)}, bf16[40,4096]{1,0:T(8,128)(2,1)S(1)}, u32[]{:S(2)}, u32[]{:S(2)}) %collective-permute-start) | collective-permute-done | bytes 327712 | tf_op jit(solution)/shard_map/ppermute | solution.py:41
  81.5 8.3 %collective-permute-done.1 = bf16[40,4096]{1,0:T(8,128)(2,1)S(1)} collective-permute-done((bf16[40,4096]{1,0:T(8,128)(2,1)S(1)}, bf16[40,4096]{1,0:T(8,128)(2,1)S(1)}, u32[]{:S(2)}, u32[]{:S(2)}) %collective-permute-start.1) | collective-permute-done | bytes 327712 | tf_op jit(solution)/shard_map/ppermute | solution.py:41
  89.8 16.6 %reduce-scatter.7.cloned.1.call-done = bf16[256,1376]{0,1:T(8,128)(2,1)} async-done(((bf16[1024,1376]{0,1:T(8,128)(2,1)}), bf16[256,1376]{0,1:T(8,128)(2,1)}) %reduce-scatter.7.cloned.1.call-update) | async-done | bytes 704528 | tf_op jit(solution)/shard_map/reduce_scatter | solution.py:37
  106.5 44.3 %reduce-scatter.9.cloned.1.call-done = bf16[256,1376]{0,1:T(8,128)(2,1)} async-done(((bf16[1024,1376]{0,1:T(8,128)(2,1)}), bf16[256,1376]{0,1:T(8,128)(2,1)}) %reduce-scatter.9.cloned.1.call-update) | async-done | bytes 704528 | tf_op jit(solution)/shard_map/reduce_scatter | solution.py:38
  150.7 2.6 fusion.22
  153.5 8.3 %collective-permute-done.3 = bf16[40,4096]{1,0:T(8,128)(2,1)S(1)} collective-permute-done((bf16[40,4096]{1,0:T(8,128)(2,1)S(1)}, bf16[40,4096]{1,0:T(8,128)(2,1)S(1)}, u32[]{:S(2)}, u32[]{:S(2)}) %collective-permute-start.3) | collective-permute-done | bytes 327712 | tf_op jit(solution)/shard_map/ppermute | solution.py:41
  161.8 8.3 %collective-permute-done.4 = bf16[40,4096]{1,0:T(8,128)(2,1)S(1)} collective-permute-done((bf16[40,4096]{1,0:T(8,128)(2,1)S(1)}, bf16[40,4096]{1,0:T(8,128)(2,1)S(1)}, u32[]{:S(2)}, u32[]{:S(2)}) %collective-permute-start.4) | collective-permute-done | bytes 327712 | tf_op jit(solution)/shard_map/ppermute | solution.py:41
  170.1 8.3 %collective-permute-done.5 = bf16[40,4096]{1,0:T(8,128)(2,1)S(1)} collective-permute-done((bf16[40,4096]{1,0:T(8,128)(2,1)S(1)}, bf16[40,4096]{1,0:T(8,128)(2,1)S(1)}, u32[]{:S(2)}, u32[]{:S(2)}) %collective-permute-start.5) | collective-permute-done | bytes 327712 | tf_op jit(solution)/shard_map/ppermute | solution.py:41
  179.1 7.6 %collective-permute-done.6 = bf16[40,4096]{1,0:T(8,128)(2,1)S(1)} collective-permute-done((bf16[40,4096]{1,0:T(8,128)(2,1)S(1)}, bf16[40,4096]{1,0:T(8,128)(2,1)S(1)}, u32[]{:S(2)}, u32[]{:S(2)}) %collective-permute-start.6) | collective-permute-done | bytes 327712 | tf_op jit(solution)/shard_map/ppermute | solution.py:41
  191.2 3.3 %all-gather.4.cloned.1.call-done = bf16[1024,1376]{0,1:T(8,128)(2,1)} async-done(((bf16[256,1376]{0,1:T(8,128)(2,1)}), bf16[1024,1376]{0,1:T(8,128)(2,1)}) %all-gather.4.cloned.1.call-update) | async-done | bytes 2818064 | tf_op jit(solution)/shard_map/all_gather | solution.py:55
  194.5 6.1 %convolution_convert_fusion.3 = bf16[1024,1024]{1,0:T(8,128)(2,1)S(1)} fusion(bf16[1024,1376]{0,1:T(8,128)(2,1)} %all-gather.4.cloned.1.call-done, bf16[1376,1024]{1,0:T(8,128)(2,1)} %param.18), kind=kOutput, calls=%fused_computation.21 | convolution fusion | flops 2886729728 | bytes 7733248 | tf_op jit(solution)/shard_map/dot_general | solution.py:56
  201.6 1.8 pad_maximum_fusion
  211.2 1.9 conditional.1
  211.2 1.9 broadcast.43
  213.1 28.2 %reduce-scatter.11.cloned.1.call-done = bf16[1,160,1024]{2,1,0:T(8,128)(2,1)} async-done(((bf16[8,160,1024]{2,1,0:T(8,128)(2,1)}), bf16[1,160,1024]{2,1,0:T(8,128)(2,1)}) %reduce-scatter.11.cloned.1.call-update) | async-done | bytes 327696 | tf_op jit(solution)/shard_map/reduce_scatter | solution.py:61
  241.4 3.6 %all-to-all-start.1 = ((bf16[4,40,1024]{2,1,0:T(8,128)(2,1)}), bf16[4,40,1024]{2,1,0:T(8,128)(2,1)S(1)}, u32[]{:S(2)}, u32[]{:S(2)}) async-start(bf16[4,40,1024]{2,1,0:T(8,128)(2,1)} %bitcast.39), calls=%async_computation.5 | async-start | bytes 655360 | tf_op jit(solution)/shard_map/all_to_all | solution.py:63
  245.0 5.5 %all-to-all-done.1 = bf16[4,40,1024]{2,1,0:T(8,128)(2,1)S(1)} async-done(((bf16[4,40,1024]{2,1,0:T(8,128)(2,1)}), bf16[4,40,1024]{2,1,0:T(8,128)(2,1)S(1)}, u32[]{:S(2)}, u32[]{:S(2)}) %all-to-all-start.1) | async-done | bytes 327712 | tf_op jit(solution)/shard_map/all_to_all | solution.py:63
  251.3 29.3 %reduce-scatter.5.cloned.1.call-done = bf16[40,4096]{1,0:T(8,128)(2,1)} async-done(((bf16[320,4096]{1,0:T(8,128)(2,1)}), bf16[40,4096]{1,0:T(8,128)(2,1)}) %reduce-scatter.5.cloned.1.call-update) | async-done | bytes 327696 | tf_op jit(solution)/shard_map/reduce_scatter | solution.py:53
  280.6 1.8 fusion.26
  (84 shorter events, 21.3 us)
Async XLA Ops:
  6.5 54.4 %copy-start = (bf16[1024,1376]{0,1:T(8,128)(2,1)S(1)}, bf16[1024,1376]{0,1:T(8,128)(2,1)}, u32[]{:S(2)}) copy-start(bf16[1024,1376]{0,1:T(8,128)(2,1)} %param.16) | copy-start | bytes 8454148
  6.5 48.8 %all-gather.6.cloned.1.call-start = ((), (), s32[]{:S(2)}) async-start(), calls=%async_computation.11 | async-start | bytes 2949120 | tf_op jit(solution)/shard_map/all_gather | solution.py:27
  21.9 84.5 %reduce-scatter.7.cloned.1.call-start = ((), (), s32[]{:S(2)}) async-start(), calls=%async_computation.7 | async-start | bytes 3522560 | tf_op jit(solution)/shard_map/reduce_scatter | solution.py:37
  66.0 84.7 %reduce-scatter.9.cloned.1.call-start = ((), (), s32[]{:S(2)}) async-start(), calls=%async_computation.8 | async-start | bytes 3522560 | tf_op jit(solution)/shard_map/reduce_scatter | solution.py:38
  73.1 105.3 %copy-start.16 = (s32[3]{0:T(128)S(1)}, s32[3]{0:T(128)}, u32[]{:S(2)}) copy-start(s32[3]{0:T(128)} %constant.94.clone.1) | copy-start | bytes 40
  73.1 121.4 %all-gather.4.cloned.1.call-start = ((), (), s32[]{:S(2)}) async-start(), calls=%async_computation.9 | async-start | bytes 3522560 | tf_op jit(solution)/shard_map/all_gather | solution.py:55
  73.2 8.3 %collective-permute-start = (bf16[40,4096]{1,0:T(8,128)(2,1)S(1)}, bf16[40,4096]{1,0:T(8,128)(2,1)S(1)}, u32[]{:S(2)}, u32[]{:S(2)}) collective-permute-start(bf16[40,4096]{1,0:T(8,128)(2,1)S(1)} %fusion.25), channel_id=1, source_target_pairs={{0,1},{1,2},{2,3},{3,4},{4,5},{5,6},{6,7},{7,0},{8,9},{9,10},{10,1... | collective-permute-start | bytes 983048 | tf_op jit(solution)/shard_map/ppermute | solution.py:41
  81.5 8.3 %collective-permute-start.1 = (bf16[40,4096]{1,0:T(8,128)(2,1)S(1)}, bf16[40,4096]{1,0:T(8,128)(2,1)S(1)}, u32[]{:S(2)}, u32[]{:S(2)}) collective-permute-start(bf16[40,4096]{1,0:T(8,128)(2,1)S(1)} %collective-permute-done), channel_id=1, source_target_pairs={{0,1},{1,2},{2,3},{3,4},{4,5},{5,6},{6,7},{7,0},{8,9},{9,10},{10,1... | collective-permute-start | bytes 983048 | tf_op jit(solution)/shard_map/ppermute | solution.py:41
  89.8 110.8 %copy-start.5 = (bf16[40,4096]{1,0:T(8,128)(2,1)}, bf16[40,4096]{1,0:T(8,128)(2,1)S(1)}, u32[]{:S(2)}) copy-start(bf16[40,4096]{1,0:T(8,128)(2,1)S(1)} %collective-permute-done.1) | copy-start | bytes 983044
  89.8 63.6 %collective-permute-start.2 = (bf16[40,4096]{1,0:T(8,128)(2,1)S(1)}, bf16[40,4096]{1,0:T(8,128)(2,1)S(1)}, u32[]{:S(2)}, u32[]{:S(2)}) collective-permute-start(bf16[40,4096]{1,0:T(8,128)(2,1)S(1)} %collective-permute-done.1), channel_id=1, source_target_pairs={{0,1},{1,2},{2,3},{3,4},{4,5},{5,6},{6,7},{7,0},{8,9},{9,10},{10,1... | collective-permute-start | bytes 983048 | tf_op jit(solution)/shard_map/ppermute | solution.py:41
  153.4 88.0 %reduce-scatter.11.cloned.1.call-start = ((), (), s32[]{:S(2)}) async-start(), calls=%async_computation.10 | async-start | bytes 2949120 | tf_op jit(solution)/shard_map/reduce_scatter | solution.py:61
  153.4 41.1 %copy-start.7 = (bf16[40,4096]{1,0:T(8,128)(2,1)}, bf16[40,4096]{1,0:T(8,128)(2,1)S(1)}, u32[]{:S(2)}) copy-start(bf16[40,4096]{1,0:T(8,128)(2,1)S(1)} %collective-permute-done.2) | copy-start | bytes 983044
  153.4 8.3 %collective-permute-start.3 = (bf16[40,4096]{1,0:T(8,128)(2,1)S(1)}, bf16[40,4096]{1,0:T(8,128)(2,1)S(1)}, u32[]{:S(2)}, u32[]{:S(2)}) collective-permute-start(bf16[40,4096]{1,0:T(8,128)(2,1)S(1)} %collective-permute-done.2), channel_id=1, source_target_pairs={{0,1},{1,2},{2,3},{3,4},{4,5},{5,6},{6,7},{7,0},{8,9},{9,10},{10,1... | collective-permute-start | bytes 983048 | tf_op jit(solution)/shard_map/ppermute | solution.py:41
  161.8 32.7 %copy-start.9 = (bf16[40,4096]{1,0:T(8,128)(2,1)}, bf16[40,4096]{1,0:T(8,128)(2,1)S(1)}, u32[]{:S(2)}) copy-start(bf16[40,4096]{1,0:T(8,128)(2,1)S(1)} %collective-permute-done.3) | copy-start | bytes 983044
  161.8 8.3 %collective-permute-start.4 = (bf16[40,4096]{1,0:T(8,128)(2,1)S(1)}, bf16[40,4096]{1,0:T(8,128)(2,1)S(1)}, u32[]{:S(2)}, u32[]{:S(2)}) collective-permute-start(bf16[40,4096]{1,0:T(8,128)(2,1)S(1)} %collective-permute-done.3), channel_id=1, source_target_pairs={{0,1},{1,2},{2,3},{3,4},{4,5},{5,6},{6,7},{7,0},{8,9},{9,10},{10,1... | collective-permute-start | bytes 983048 | tf_op jit(solution)/shard_map/ppermute | solution.py:41
  170.1 24.4 %copy-start.11 = (bf16[40,4096]{1,0:T(8,128)(2,1)}, bf16[40,4096]{1,0:T(8,128)(2,1)S(1)}, u32[]{:S(2)}) copy-start(bf16[40,4096]{1,0:T(8,128)(2,1)S(1)} %collective-permute-done.4) | copy-start | bytes 983044
  170.1 8.3 %collective-permute-start.5 = (bf16[40,4096]{1,0:T(8,128)(2,1)S(1)}, bf16[40,4096]{1,0:T(8,128)(2,1)S(1)}, u32[]{:S(2)}, u32[]{:S(2)}) collective-permute-start(bf16[40,4096]{1,0:T(8,128)(2,1)S(1)} %collective-permute-done.4), channel_id=1, source_target_pairs={{0,1},{1,2},{2,3},{3,4},{4,5},{5,6},{6,7},{7,0},{8,9},{9,10},{10,1... | collective-permute-start | bytes 983048 | tf_op jit(solution)/shard_map/ppermute | solution.py:41
  178.4 16.1 %copy-start.13 = (bf16[40,4096]{1,0:T(8,128)(2,1)}, bf16[40,4096]{1,0:T(8,128)(2,1)S(1)}, u32[]{:S(2)}) copy-start(bf16[40,4096]{1,0:T(8,128)(2,1)S(1)} %collective-permute-done.5) | copy-start | bytes 983044
  178.4 8.3 %collective-permute-start.6 = (bf16[40,4096]{1,0:T(8,128)(2,1)S(1)}, bf16[40,4096]{1,0:T(8,128)(2,1)S(1)}, u32[]{:S(2)}, u32[]{:S(2)}) collective-permute-start(bf16[40,4096]{1,0:T(8,128)(2,1)S(1)} %collective-permute-done.5), channel_id=1, source_target_pairs={{0,1},{1,2},{2,3},{3,4},{4,5},{5,6},{6,7},{7,0},{8,9},{9,10},{10,1... | collective-permute-start | bytes 983048 | tf_op jit(solution)/shard_map/ppermute | solution.py:41
  203.3 4.7 %copy-start.8 = (bf16[40,4096]{1,0:T(8,128)(2,1)S(1)}, bf16[40,4096]{1,0:T(8,128)(2,1)}, u32[]{:S(2)}) copy-start(bf16[40,4096]{1,0:T(8,128)(2,1)} %copy-done.7) | copy-start | bytes 983044
  203.3 5.5 %copy-start.6 = (bf16[40,4096]{1,0:T(8,128)(2,1)S(1)}, bf16[40,4096]{1,0:T(8,128)(2,1)}, u32[]{:S(2)}) copy-start(bf16[40,4096]{1,0:T(8,128)(2,1)} %copy-done.5) | copy-start | bytes 983044
  203.4 77.2 %reduce-scatter.5.cloned.1.call-start = ((), (), s32[]{:S(2)}) async-start(), calls=%async_computation.6 | async-start | bytes 2949120 | tf_op jit(solution)/shard_map/reduce_scatter | solution.py:53
  213.1 69.3 %copy-start.1 = (bf16[1024,1376]{0,1:T(8,128)(2,1)S(1)}, bf16[1024,1376]{0,1:T(8,128)(2,1)}, u32[]{:S(2)}) copy-start(bf16[1024,1376]{0,1:T(8,128)(2,1)} %param.16) | copy-start | bytes 8454148
  241.4 9.2 %all-to-all-start.1 = ((bf16[4,40,1024]{2,1,0:T(8,128)(2,1)}), bf16[4,40,1024]{2,1,0:T(8,128)(2,1)S(1)}, u32[]{:S(2)}, u32[]{:S(2)}) async-start(bf16[4,40,1024]{2,1,0:T(8,128)(2,1)} %bitcast.39), calls=%async_computation.5 | async-start | bytes 655360 | tf_op jit(solution)/shard_map/all_to_all | solution.py:63
  (7 other events, 19.9 us)
Sparse Core Ops, SparseCore 0:
  22.0 33.2 all-gather.5
  66.1 40.3 reduce-scatter.6
  109.5 41.1 reduce-scatter.8
  153.5 40.9 all-gather.3
  203.5 37.8 reduce-scatter.10
  243.5 37.0 reduce-scatter.4
